TPU v7x, 256 devices: a whole 4x4x8 slice. The times are simulated.
256 devices in a mesh: frag: 16 (over x, y), tile: 8 (over z), ka: 2 (over core).
Axes of the slice: x: 4, y: 4, z: 8, core: 2. Of those that a mesh axis runs over, the one named last changes fastest.
Arguments:
- sizes: int32 [128], replicated, may hold values from 40 to 400
- neighbors: int32 [128, 4], P('frag'), may hold values from 0 to 127, as said below
- slot_fragment: int32 [128], replicated, may hold values from 0 to 127, as said below
- density: bfloat16 [128, 512, 512], P('frag', ('tile', 'ka')), may hold values from -6 to 6
- hcore: bfloat16 [128, 512, 512], P('frag', ('tile', 'ka')), may hold values from -3 to 3
- integrals: bfloat16 [128, 32, 512, 512], P('frag', ('tile', 'ka')), may hold values from -0.15625 to 0.15625
- couple: bfloat16 [128, 4, 512, 512], P('frag', None, ('tile', 'ka')), may hold values from -2.390625 to 2.390625
Outputs:
- fock: float32 [128, 512, 512], P('frag', ('tile', 'ka'))
Inputs may be any that keep to these rules, and one draw needn't show every extreme that they name: `neighbors`: fragment f belongs to group f // 8; each entry names a fragment other than f itself, belonging to the same group or to the next group on either side. `slot_fragment`: A permutation of the fragments; slots s with s // 8 == h form balanced group h; no group's fragments fill more than 1 slots of one balanced group, and some pair of groups reaches 1.
All inputs are finite; a program needn't handle non-finite values.
Results may differ from a plain program's by a relative error of at most 0.002.
Values may be sent and summed in bfloat16 or wider, within the bound.
No kernel may reach another device: no remote copies, remote signals or barrier semaphores. Data moves between devices by JAX's collectives and lax.ppermute only.
A program may use at most 64 MiB of HBM per device.

v0:
```python
import functools

import jax
import jax.numpy as jnp
from jax import lax
from jax.experimental import pallas as pl
from jax.experimental.pallas import tpu as pltpu
from jax.sharding import PartitionSpec as P


F16 = jnp.float16
F32 = jnp.float32
BF16 = jnp.bfloat16
TILE = 128
TILES = 4
CLASSES = (16, 19, 32)
PAIR_SCALE = 0.25
SUM_SCALE = 0.03125
SMEM = pl.BlockSpec(memory_space=pltpu.SMEM)
VMEM = pl.BlockSpec(memory_space=pltpu.VMEM)


def tiles_of(size):
    return (size + (TILE - 1)) // TILE


def held_slot(sizes, slots, first, k):
    frag = slots[first + k]
    return frag, tiles_of(sizes[frag])


def masked_rows(value, size, first_row, first_col):
    rows = first_row + lax.broadcasted_iota(jnp.int32, value.shape, 0)
    cols = first_col + lax.broadcasted_iota(jnp.int32, value.shape, 1)
    return jnp.where((rows < size) & (cols < size), value, jnp.zeros_like(value))


def send_body(where, sizes, slots, density, out, kind, pack, back, targets):
    per_group, slab, width = density.shape
    groups = out.shape[0]
    first = where[0] * per_group
    widest = jnp.int32(0)
    for group in range(groups):
        total = jnp.int32(0)
        for k in range(per_group):
            frag = slots[group * per_group + k]
            total = total + tiles_of(sizes[frag])
            local = frag - first
            inside = (local >= 0) & (local < per_group)
            targets[jnp.where(inside, local, per_group)] = group
        widest = jnp.maximum(widest, total)
    index = jnp.int32(0)
    for limit in CLASSES[:-1]:
        index = index + (widest > limit).astype(jnp.int32)
    kind[0] = index
    for place in range(pack.shape[0]):
        pack[place] = 0
    for place in range(back.shape[0]):
        back[place] = 0
    offset = jnp.int32(0)
    for k in range(per_group):
        frag, count = held_slot(sizes, slots, first, k)
        source = frag // per_group
        for c in range(TILES):
            valid = c < count
            pack[jnp.where(valid, offset + c, pack.shape[0] - 1)] = source * TILES + c
            back[source * TILES + c] = jnp.where(valid, offset + c, 0)
        offset = offset + count
    for j in range(per_group):
        rows = masked_rows(
            density[j].astype(F32), sizes[first + j], where[1] * slab, 0
        ).astype(BF16)
        for c in range(width // TILE):
            out[targets[j], c] = rows[:, c * TILE : (c + 1) * TILE]


def fock_body(
    where, sizes, slots, gathered, factors, keep, send, vectors, dense, halved, total, arrived
):
    per_group = factors.shape[0]
    first = where[0] * per_group
    chip = where[3]
    chips, capacity = keep.shape[:2]
    mine = where[2]
    slab = gathered.shape[2]
    chol = factors.shape[1]
    right = (chip + 1) % chips
    left = (chip + chips - 1) % chips
    half = chips // 2

    def copies(k, tiles):
        extent = tiles * TILE
        used = pl.ds(0, extent)
        return [
            pltpu.make_async_copy(
                factors.at[k, q, used, used],
                vectors.at[k, used, pl.ds(q * extent, extent)],
                arrived.at[k, q],
            )
            for q in range(chol)
        ]

    def run(k, offset, tiles):
        extent = tiles * TILE
        pieces = [(r, c) for r in range(extent // slab) for c in range(tiles)]
        rows = lambda r: slice(r * slab, (r + 1) * slab)
        cols = lambda c: slice(c * TILE, (c + 1) * TILE)
        for r, c in pieces:
            dense[rows(r), cols(c)] = gathered[r, offset + c]
        for copy in copies(k, tiles):
            copy.wait()
        block = dense[:extent, :extent]
        for q in range(chol):
            span = slice(q * extent, (q + 1) * extent)
            product = jnp.dot(vectors[k, :extent, span], block, preferred_element_type=F32)
            halved[:extent, span] = (-0.5 * product).astype(BF16)
        wide = slice(0, chol * extent)
        total[:extent, :extent] = lax.dot_general(
            halved[:extent, wide],
            vectors[k, :extent, wide],
            (((1,), (1,)), ((), ())),
            preferred_element_type=F32,
        )
        factor = lambda q, r, c: vectors[k, rows(r), cols(q * tiles + c)].astype(F32)
        sums = [jnp.zeros((slab, TILE), F32) for _ in range(chol)]
        for r, c in pieces:
            part = dense[rows(r), cols(c)].astype(F32)
            sums = [value + factor(q, r, c) * part for q, value in enumerate(sums)]
        coulomb = [jnp.sum(value, keepdims=True) for value in sums]

        def finish(r, c):
            value = total[rows(r), cols(c)]
            for q in range(chol):
                value = value + coulomb[q] * factor(q, r, c)
            return value

        first_core = mine == 0
        for target in range(extent // (2 * slab)):
            same = (target + chip) % 2 == 0
            own_row = (target // 2 + half - chip // 2) % half
            up_row = half + (target // 2 + half - right // 2) % half
            down_row = half + (target // 2 + half - left // 2) % half
            for c in range(tiles):
                place = offset + c
                far_row = jnp.where(place < (capacity + 1) // 2, up_row, down_row)
                row = jnp.where(same, own_row, far_row)
                even = finish(2 * target, c)
                odd = finish(2 * target + 1, c)
                keep[row, place] = jnp.where(first_core, even, odd)
                send[row, place] = jnp.where(first_core, odd, even)

    for k in range(per_group):
        _, count = held_slot(sizes, slots, first, k)
        for tiles in range(1, TILES + 1):
            pl.when(count == tiles)(lambda: [copy.start() for copy in copies(k, tiles)] and None)

    def slot(k, offset):
        _, count = held_slot(sizes, slots, first, k)
        for tiles in range(1, TILES + 1):
            pl.when(count == tiles)(functools.partial(run, k, offset, tiles))
        return offset + count

    lax.fori_loop(0, per_group, slot, jnp.int32(0))


def base_body(where, sizes, neighbors, low, own, high, hcore, couple, out):
    per_group, slab, _ = own.shape
    first = where[0] * per_group
    row = where[1] * slab
    listed = neighbors.shape[1]

    def fragment(j, carry):
        out[j] = hcore[j].astype(F32)
        for k in range(listed):
            near = neighbors[j, k]
            size = sizes[near]
            weight = couple[j, k].astype(F32)
            place = near - first
            group = jnp.where(place < 0, 0, jnp.where(place < per_group, 1, 2))
            position = place - (group - 1) * per_group

            def add(source):
                rows = masked_rows(source[position].astype(F32), size, row, 0)
                out[j] += weight * rows

            for side, source in enumerate((low, own, high)):
                pl.when(group == side)(functools.partial(add, source))
        return carry

    lax.fori_loop(0, per_group, fragment, 0)


def local(sizes, neighbors, slot_fragment, density, hcore, integrals, couple):
    groups = lax.axis_size("frag")
    cores = lax.axis_size("ka")
    chips = lax.axis_size("tile")
    group = lax.axis_index("frag")
    core = lax.axis_index("ka")
    lane = lax.axis_index("tile") * cores + core
    per_group, slab, width = density.shape
    chol = integrals.shape[1]
    where = jnp.stack([group, lane, core, lax.axis_index("tile")]).astype(jnp.int32)
    shift = lambda value, by: lax.ppermute(
        value, "tile", [(i, (i + by) % chips) for i in range(chips)]
    )

    block = (groups, TILES, slab, TILE)
    table = lambda count: jax.ShapeDtypeStruct((count,), jnp.int32)
    outgoing, kind, pack, back, targets = pl.pallas_call(
        send_body,
        out_shape=(
            jax.ShapeDtypeStruct(block, BF16),
            table(1),
            table(per_group * TILES + 1),
            table(groups * TILES),
            table(per_group + 1),
        ),
        in_specs=[SMEM, SMEM, SMEM, VMEM],
        out_specs=(VMEM, SMEM, SMEM, SMEM, SMEM),
        name="send",
    )(where, sizes, slot_fragment, density)
    received = lax.all_to_all(outgoing, "frag", split_axis=0, concat_axis=0, tiled=True)

    def balanced(capacity, received):
        split = (capacity + 1) // 2
        half_chips = chips // 2
        flat = received.reshape(groups * TILES, slab, TILE)
        packed = jnp.take(flat, pack[:capacity], axis=0, mode="clip").astype(F16)
        gathered = lax.all_gather(packed, ("tile", "ka"), axis=0, tiled=False).astype(BF16)
        half = jax.ShapeDtypeStruct((chips, capacity, slab, TILE), F32)
        keep, send = pl.pallas_call(
            fock_body,
            out_shape=(half, half),
            in_specs=[SMEM] * 3 + [VMEM, pl.BlockSpec(memory_space=pl.ANY)],
            out_specs=(VMEM, VMEM),
            scratch_shapes=[
                pltpu.VMEM((per_group, width, chol * width), BF16),
                pltpu.VMEM((width, width), BF16),
                pltpu.VMEM((width, chol * width), BF16),
                pltpu.VMEM((width, width), F32),
                pltpu.SemaphoreType.DMA((per_group, chol)),
            ],
            compiler_params=pltpu.CompilerParams(
                vmem_limit_bytes=(20 + capacity // 2) << 20
            ),
            name="fock",
        )(where, sizes, slot_fragment, gathered, integrals)
        other = lax.ppermute(send, "ka", [(0, 1), (1, 0)])
        pair = (keep + other) * PAIR_SCALE
        up = shift(pair[half_chips:, :split].astype(F16), 1)
        down = shift(pair[half_chips:, split:].astype(F16), -1)
        own = pair[:half_chips] + jnp.concatenate([up, down], axis=1).astype(F32)
        far = own.astype(F16)
        slab_rows, far = lax.optimization_barrier((density, far))
        moved = [shift(far[step], 2 * step) for step in range(1, half_chips)]
        low = lax.ppermute(slab_rows, "frag", [(i, i + 1) for i in range(groups - 1)])
        high = lax.ppermute(slab_rows, "frag", [(i + 1, i) for i in range(groups - 1)])
        total = own[0] + sum(part.astype(F32) for part in moved)
        total = lax.optimization_barrier((total * (SUM_SCALE / PAIR_SCALE)).astype(F16))
        return jnp.take(total, back, axis=0, mode="clip"), low, high

    branches = [functools.partial(balanced, capacity) for capacity in CLASSES]
    summed, low, high = lax.switch(kind[0], branches, received)
    summed = summed.reshape(block)
    returned = lax.all_to_all(summed, "frag", split_axis=0, concat_axis=0, tiled=True)
    base = pl.pallas_call(
        base_body,
        out_shape=jax.ShapeDtypeStruct(density.shape, F32),
        in_specs=[SMEM] * 3 + [VMEM] * 5,
        out_specs=VMEM,
        name="base",
    )(where, sizes, neighbors, low, density, high, hcore, couple)
    picked = jnp.take(returned, targets[:per_group], axis=0, mode="clip")
    two_body = picked.astype(F32).transpose(0, 2, 1, 3).reshape(density.shape)
    own_sizes = lax.dynamic_slice_in_dim(sizes, group * per_group, per_group)[:, None, None]
    rows = lane * slab + lax.broadcasted_iota(jnp.int32, density.shape, 1)
    cols = lax.broadcasted_iota(jnp.int32, density.shape, 2)
    keep = (rows < own_sizes) & (cols < own_sizes)
    return jnp.where(keep, base + two_body * (1.0 / SUM_SCALE), 0.0)


def solution(mesh):
    return jax.shard_map(
        local,
        mesh=mesh,
        in_specs=(
            P(),
            P("frag", None),
            P(),
            P("frag", ("tile", "ka"), None),
            P("frag", ("tile", "ka"), None),
            P("frag", ("tile", "ka"), None, None),
            P("frag", None, ("tile", "ka"), None),
        ),
        out_specs=P("frag", ("tile", "ka"), None),
        check_vma=False,
    )
```

profile of v0, /device:TPU:2, one launch (start us, length us, event | category | flops | bytes accessed | tf_op | source)
XLA Modules:
  0.0 110.7 jit_solution(5130221571659568556)
XLA Ops:
  0.1 2.8 %send.1 = (bf16[16,4,32,128]{3,2,1,0:T(8,128)(2,1)}, s32[1]{0:T(128)}, s32[33]{0:T(128)S(1)}, s32[64]{0:T(128)S(1)}, s32[9]{0:T(128)}) custom-call(s32[4]{0:T(128)S(1)} %pad_add_fusion.where, s32[128]{0:T(128)} %sizes.3, s32[128]{0:T(128)} %slots.1, bf16[8,32,512]{2,1,0:T(8,128)(2,1)} %own.1), custom_call_target="tpu_custom_call" | custom-call | tf_op jit(solution)/shard_map/send/pallas_call | solution.py:209
  2.9 7.5 %all-to-all-start = ((bf16[16,4,32,128]{3,2,1,0:T(8,128)(2,1)}), bf16[16,4,32,128]{3,2,1,0:T(8,128)(2,1)S(1)}, u32[]{:S(2)}, u32[]{:S(2)}) async-start(bf16[16,4,32,128]{3,2,1,0:T(8,128)(2,1)} %get-tuple-element.98), calls=%async_computation | async-start | bytes 1048576 | tf_op jit(solution)/shard_map/all_to_all | solution.py:222
  10.9 8.8 %all-to-all-done = bf16[16,4,32,128]{3,2,1,0:T(8,128)(2,1)S(1)} async-done(((bf16[16,4,32,128]{3,2,1,0:T(8,128)(2,1)}), bf16[16,4,32,128]{3,2,1,0:T(8,128)(2,1)S(1)}, u32[]{:S(2)}, u32[]{:S(2)}) %all-to-all-start) | async-done | bytes 524320 | tf_op jit(solution)/shard_map/all_to_all | solution.py:222
  19.7 73.7 %conditional.1 = (f16[64,32,128]{2,1,0:T(8,128)(2,1)}, bf16[8,32,512]{2,1,0:T(8,128)(2,1)}, bf16[8,32,512]{2,1,0:T(8,128)(2,1)}) conditional(s32[]{:T(128)} %bitcast.22, (bf16[16,4,32,128]{3,2,1,0:T(8,128)(2,1)S(1)}, s32[33]{0:T(128)S(1)}, s32[4]{0:T(128)S(1)}, s32[128]{0:T(128)}, s32[128]{0:T(128)}, ...), branch_computations={%region_0.1_spmd, %region_1.2_spmd, %region_2.3_spmd} | conditional | flops 8521728 | bytes 101987536 | solution.py:263
  20.4 27.1 %all-gather.7 = f16[304,32,128]{2,1,0:T(8,128)(2,1)S(1)} all-gather(f16[19,32,128]{2,1,0:T(8,128)(2,1)S(1)} %convert_element_type.94), channel_id=3, replica_groups=mesh['frag'=16,'tile'=8,'ka'=2] {'tile','ka'}, dimensions={0}, use_global_device_ids=true | all-gather | bytes 2646016 | tf_op jit(solution)/shard_map/cond/branch_1_fun/all_gather | solution.py:229
  48.1 7.0 %fock.4 = (f32[8,19,32,128]{3,2,1,0:T(8,128)S(1)}, f32[8,19,32,128]{3,2,1,0:T(8,128)S(1)}) custom-call(s32[4]{0:T(128)S(1)} %get-tuple-element.65.where, s32[128]{0:T(128)S(1)} %copy-done.6, s32[128]{0:T(128)S(1)} %copy-done.9, bf16[16,19,32,128]{3,2,1,0:T(8,128)(2,1)S(1)} %bitcast.67, bf16[8,2,512,512]{3,2,1,0:T(8,128)(2,1)} %get-tuple-element.70.factors), custom_call_target="tpu_custom_call" | custom-call | tf_op jit(solution)/shard_map/cond/branch_1_fun/fock/pallas_call | solution.py:231
  55.5 4.4 %collective-permute-done = f32[8,19,32,128]{3,2,1,0:T(8,128)S(1)} collective-permute-done((f32[8,19,32,128]{3,2,1,0:T(8,128)S(1)}, f32[8,19,32,128]{3,2,1,0:T(8,128)S(1)}, u32[]{:S(2)}, u32[]{:S(2)}) %collective-permute-start) | collective-permute-done | bytes 2490400 | tf_op jit(solution)/shard_map/cond/branch_1_fun/ppermute | solution.py:248
  60.6 1.2 %collective-permute-start.1 = (f16[4,10,32,128]{3,2,1,0:T(8,128)(2,1)S(1)}, f16[4,10,32,128]{3,2,1,0:T(8,128)(2,1)S(1)}, u32[]{:S(2)}, u32[]{:S(2)}) collective-permute-start(f16[4,10,32,128]{3,2,1,0:T(8,128)(2,1)S(1)} %slice.101), channel_id=1, source_target_pairs={{0,2},{2,4},{4,6},{6,8},{8,10},{10,12},{12,14},{14,0},{1,3},{3,5},... | collective-permute-start | bytes 983048 | tf_op jit(solution)/shard_map/cond/branch_1_fun/ppermute | solution.py:203
  61.9 2.2 %collective-permute-start.2 = (f16[4,9,32,128]{3,2,1,0:T(8,128)(2,1)S(1)}, f16[4,9,32,128]{3,2,1,0:T(8,128)(2,1)S(1)}, u32[]{:S(2)}, u32[]{:S(2)}) collective-permute-start(f16[4,9,32,128]{3,2,1,0:T(8,128)(2,1)S(1)} %slice.102), channel_id=1, source_target_pairs={{0,14},{2,0},{4,2},{6,4},{8,6},{10,8},{12,10},{14,12},{1,15},{3,1}... | collective-permute-start | bytes 884744 | tf_op jit(solution)/shard_map/cond/branch_1_fun/ppermute | solution.py:203
  64.1 6.9 %collective-permute-done.2 = f16[4,9,32,128]{3,2,1,0:T(8,128)(2,1)S(1)} collective-permute-done((f16[4,9,32,128]{3,2,1,0:T(8,128)(2,1)S(1)}, f16[4,9,32,128]{3,2,1,0:T(8,128)(2,1)S(1)}, u32[]{:S(2)}, u32[]{:S(2)}) %collective-permute-start.2) | collective-permute-done | bytes 294944 | tf_op jit(solution)/shard_map/cond/branch_1_fun/ppermute | solution.py:203
  71.0 0.9 collective-permute-done.1
  72.6 3.0 %collective-permute-start.4 = (f16[19,32,128]{2,1,0:T(8,128)(2,1)S(1)}, f16[19,32,128]{2,1,0:T(8,128)(2,1)S(1)}, u32[]{:S(2)}, u32[]{:S(2)}) collective-permute-start(f16[19,32,128]{2,1,0:T(8,128)(2,1)S(1)} %get-tuple-element.124), channel_id=1, source_target_pairs={{0,8},{2,10},{4,12},{6,14},{8,0},{10,2},{12,4},{14,6},{1,9},{3,11}... | collective-permute-start | bytes 466952 | tf_op jit(solution)/shard_map/cond/branch_1_fun/ppermute | solution.py:203
  75.6 3.8 %collective-permute-start.5 = (f16[19,32,128]{2,1,0:T(8,128)(2,1)S(1)}, f16[19,32,128]{2,1,0:T(8,128)(2,1)S(1)}, u32[]{:S(2)}, u32[]{:S(2)}) collective-permute-start(f16[19,32,128]{2,1,0:T(8,128)(2,1)S(1)} %get-tuple-element.123), channel_id=1, source_target_pairs={{0,12},{2,14},{4,0},{6,2},{8,4},{10,6},{12,8},{14,10},{1,13},{3,15... | collective-permute-start | bytes 466952 | tf_op jit(solution)/shard_map/cond/branch_1_fun/ppermute | solution.py:203
  79.4 1.9 %collective-permute-start.6 = (bf16[8,32,512]{2,1,0:T(8,128)(2,1)S(1)}, bf16[8,32,512]{2,1,0:T(8,128)(2,1)}, u32[]{:S(2)}, u32[]{:S(2)}) collective-permute-start(bf16[8,32,512]{2,1,0:T(8,128)(2,1)S(1)} %copy-done.2), channel_id=1, source_target_pairs={{0,16},{16,32},{32,48},{48,64},{64,80},{80,96},{96,112},{112,128},... | collective-permute-start | bytes 786440 | tf_op jit(solution)/shard_map/cond/branch_1_fun/ppermute | solution.py:256
  81.3 6.0 %collective-permute-start.7 = (bf16[8,32,512]{2,1,0:T(8,128)(2,1)S(1)}, bf16[8,32,512]{2,1,0:T(8,128)(2,1)}, u32[]{:S(2)}, u32[]{:S(2)}) collective-permute-start(bf16[8,32,512]{2,1,0:T(8,128)(2,1)S(1)} %copy-done.2), channel_id=1, source_target_pairs={{16,0},{32,16},{48,32},{64,48},{80,64},{96,80},{112,96},{128,112},... | collective-permute-start | bytes 786440 | tf_op jit(solution)/shard_map/cond/branch_1_fun/ppermute | solution.py:257
  87.4 4.0 %collective-permute-done.5 = f16[19,32,128]{2,1,0:T(8,128)(2,1)S(1)} collective-permute-done((f16[19,32,128]{2,1,0:T(8,128)(2,1)S(1)}, f16[19,32,128]{2,1,0:T(8,128)(2,1)S(1)}, u32[]{:S(2)}, u32[]{:S(2)}) %collective-permute-start.5) | collective-permute-done | bytes 155680 | tf_op jit(solution)/shard_map/cond/branch_1_fun/ppermute | solution.py:203
  91.5 1.5 %gather_fusion.1 = f16[64,32,128]{2,1,0:T(8,128)(2,1)} fusion(f16[19,32,128]{2,1,0:T(8,128)(2,1)S(1)} %fusion.5, s32[1024]{0:T(1024)S(1)} %pad_clamp_fusion.2), kind=kCustom, calls=%fused_computation.3 | custom fusion | bytes 1048832 | tf_op jit(solution)/shard_map/cond/branch_1_fun/jit(_take)/gather | solution.py:260
  93.5 6.2 %all-to-all-start.1 = ((f16[16,4,32,128]{3,2,1,0:T(8,128)(2,1)}), f16[16,4,32,128]{3,2,1,0:T(8,128)(2,1)S(1)}, u32[]{:S(2)}, u32[]{:S(2)}) async-start(f16[16,4,32,128]{3,2,1,0:T(8,128)(2,1)} %bitcast.23), calls=%async_computation.1 | async-start | bytes 1048576 | tf_op jit(solution)/shard_map/all_to_all | solution.py:265
  99.7 0.7 copy.11.neighbors
  100.4 0.7 dynamic_slice.3
  101.1 3.5 %base.1 = f32[8,32,512]{2,1,0:T(8,128)} custom-call(s32[4]{0:T(128)S(1)} %pad_add_fusion.where, s32[128]{0:T(128)S(1)} %copy-done.4, s32[8,4]{1,0:T(8,128)} %copy.11.neighbors, bf16[8,32,512]{2,1,0:T(8,128)(2,1)} %get-tuple-element.101.low, bf16[8,32,512]{2,1,0:T(8,128)(2,1)} %own.1, bf16[8,32,512]{2,1,0:T(8,128)(2,1)} %get-tuple-element.102.high, ...), custom_call_target="tpu_custom_call" | custom-call | tf_op jit(solution)/shard_map/base/pallas_call | solution.py:266
  104.6 3.4 %all-to-all-done.1 = f16[16,4,32,128]{3,2,1,0:T(8,128)(2,1)S(1)} async-done(((f16[16,4,32,128]{3,2,1,0:T(8,128)(2,1)}), f16[16,4,32,128]{3,2,1,0:T(8,128)(2,1)S(1)}, u32[]{:S(2)}, u32[]{:S(2)}) %all-to-all-start.1) | async-done | bytes 524320 | tf_op jit(solution)/shard_map/all_to_all | solution.py:265
  108.0 0.7 gather_fusion.6
  108.7 2.0 %fusion.9 = f32[8,32,512]{2,1,0:T(8,128)} fusion(f32[8,32,512]{2,1,0:T(8,128)} %base.1, s32[8]{0:T(128)S(1)} %dynamic_slice.3, s32[32]{0:T(128)S(1)} %iota_add_fusion, f16[8,4,32,128]{3,2,1,0:T(8,128)(2,1)S(1)} %gather_fusion.6), kind=kLoop, calls=%fused_computation.41 | loop fusion | flops 917504 | bytes 1310880 | tf_op jit(solution)/shard_map/jit(_where)/select_n | solution.py:279
  (32 shorter events, 3.4 us)
Async XLA Ops:
  2.9 16.8 %all-to-all-start = ((bf16[16,4,32,128]{3,2,1,0:T(8,128)(2,1)}), bf16[16,4,32,128]{3,2,1,0:T(8,128)(2,1)S(1)}, u32[]{:S(2)}, u32[]{:S(2)}) async-start(bf16[16,4,32,128]{3,2,1,0:T(8,128)(2,1)} %get-tuple-element.98), calls=%async_computation | async-start | bytes 1048576 | tf_op jit(solution)/shard_map/all_to_all | solution.py:222
  19.7 80.0 %copy-start.11 = (s32[8,4]{0,1:T(4,128)S(1)}, s32[8,4]{0,1:T(4,128)}, u32[]{:S(2)}) copy-start(s32[8,4]{0,1:T(4,128)} %param.11) | copy-start | bytes 388
  19.7 81.4 %copy-start.12 = (s32[9]{0:T(128)S(1)}, s32[9]{0:T(128)}, u32[]{:S(2)}) copy-start(s32[9]{0:T(128)} %get-tuple-element.104) | copy-start | bytes 112
  19.7 81.4 %copy-start.4 = (s32[128]{0:T(128)S(1)}, s32[128]{0:T(128)}, u32[]{:S(2)}) copy-start(s32[128]{0:T(128)} %sizes.3) | copy-start | bytes 1540
  47.4 0.7 copy-start.6
  47.4 0.7 copy-start.9
  55.1 4.8 %collective-permute-start = (f32[8,19,32,128]{3,2,1,0:T(8,128)S(1)}, f32[8,19,32,128]{3,2,1,0:T(8,128)S(1)}, u32[]{:S(2)}, u32[]{:S(2)}) collective-permute-start(f32[8,19,32,128]{3,2,1,0:T(8,128)S(1)} %get-tuple-element.72), channel_id=1, source_target_pairs={{0,1},{1,0},{2,3},{3,2},{4,5},{5,4},{6,7},{7,6},{8,9},{9,8},{10,11... | collective-permute-start | bytes 7471112 | tf_op jit(solution)/shard_map/cond/branch_1_fun/ppermute | solution.py:248
  60.6 11.3 %collective-permute-start.1 = (f16[4,10,32,128]{3,2,1,0:T(8,128)(2,1)S(1)}, f16[4,10,32,128]{3,2,1,0:T(8,128)(2,1)S(1)}, u32[]{:S(2)}, u32[]{:S(2)}) collective-permute-start(f16[4,10,32,128]{3,2,1,0:T(8,128)(2,1)S(1)} %slice.101), channel_id=1, source_target_pairs={{0,2},{2,4},{4,6},{6,8},{8,10},{10,12},{12,14},{14,0},{1,3},{3,5},... | collective-permute-start | bytes 983048 | tf_op jit(solution)/shard_map/cond/branch_1_fun/ppermute | solution.py:203
  61.9 9.1 %collective-permute-start.2 = (f16[4,9,32,128]{3,2,1,0:T(8,128)(2,1)S(1)}, f16[4,9,32,128]{3,2,1,0:T(8,128)(2,1)S(1)}, u32[]{:S(2)}, u32[]{:S(2)}) collective-permute-start(f16[4,9,32,128]{3,2,1,0:T(8,128)(2,1)S(1)} %slice.102), channel_id=1, source_target_pairs={{0,14},{2,0},{4,2},{6,4},{8,6},{10,8},{12,10},{14,12},{1,15},{3,1}... | collective-permute-start | bytes 884744 | tf_op jit(solution)/shard_map/cond/branch_1_fun/ppermute | solution.py:203
  71.9 7.5 %copy-start.2 = (bf16[8,32,512]{2,1,0:T(8,128)(2,1)S(1)}, bf16[8,32,512]{2,1,0:T(8,128)(2,1)}, u32[]{:S(2)}) copy-start(bf16[8,32,512]{2,1,0:T(8,128)(2,1)} %get-tuple-element.76) | copy-start | bytes 786436 | tf_op jit(solution)/shard_map/cond
  72.3 15.1 %collective-permute-start.3 = (f16[19,32,128]{2,1,0:T(8,128)(2,1)S(1)}, f16[19,32,128]{2,1,0:T(8,128)(2,1)S(1)}, u32[]{:S(2)}, u32[]{:S(2)}) collective-permute-start(f16[19,32,128]{2,1,0:T(8,128)(2,1)S(1)} %get-tuple-element.122), channel_id=1, source_target_pairs={{0,4},{2,6},{4,8},{6,10},{8,12},{10,14},{12,0},{14,2},{1,5},{3,7},... | collective-permute-start | bytes 466952 | tf_op jit(solution)/shard_map/cond/branch_1_fun/ppermute | solution.py:203
  72.6 14.8 %collective-permute-start.4 = (f16[19,32,128]{2,1,0:T(8,128)(2,1)S(1)}, f16[19,32,128]{2,1,0:T(8,128)(2,1)S(1)}, u32[]{:S(2)}, u32[]{:S(2)}) collective-permute-start(f16[19,32,128]{2,1,0:T(8,128)(2,1)S(1)} %get-tuple-element.124), channel_id=1, source_target_pairs={{0,8},{2,10},{4,12},{6,14},{8,0},{10,2},{12,4},{14,6},{1,9},{3,11}... | collective-permute-start | bytes 466952 | tf_op jit(solution)/shard_map/cond/branch_1_fun/ppermute | solution.py:203
  75.6 15.7 %collective-permute-start.5 = (f16[19,32,128]{2,1,0:T(8,128)(2,1)S(1)}, f16[19,32,128]{2,1,0:T(8,128)(2,1)S(1)}, u32[]{:S(2)}, u32[]{:S(2)}) collective-permute-start(f16[19,32,128]{2,1,0:T(8,128)(2,1)S(1)} %get-tuple-element.123), channel_id=1, source_target_pairs={{0,12},{2,14},{4,0},{6,2},{8,4},{10,6},{12,8},{14,10},{1,13},{3,15... | collective-permute-start | bytes 466952 | tf_op jit(solution)/shard_map/cond/branch_1_fun/ppermute | solution.py:203
  79.4 13.6 %collective-permute-start.6 = (bf16[8,32,512]{2,1,0:T(8,128)(2,1)S(1)}, bf16[8,32,512]{2,1,0:T(8,128)(2,1)}, u32[]{:S(2)}, u32[]{:S(2)}) collective-permute-start(bf16[8,32,512]{2,1,0:T(8,128)(2,1)S(1)} %copy-done.2), channel_id=1, source_target_pairs={{0,16},{16,32},{32,48},{48,64},{64,80},{80,96},{96,112},{112,128},... | collective-permute-start | bytes 786440 | tf_op jit(solution)/shard_map/cond/branch_1_fun/ppermute | solution.py:256
  81.3 11.7 %collective-permute-start.7 = (bf16[8,32,512]{2,1,0:T(8,128)(2,1)S(1)}, bf16[8,32,512]{2,1,0:T(8,128)(2,1)}, u32[]{:S(2)}, u32[]{:S(2)}) collective-permute-start(bf16[8,32,512]{2,1,0:T(8,128)(2,1)S(1)} %copy-done.2), channel_id=1, source_target_pairs={{16,0},{32,16},{48,32},{64,48},{80,64},{96,80},{112,96},{128,112},... | collective-permute-start | bytes 786440 | tf_op jit(solution)/shard_map/cond/branch_1_fun/ppermute | solution.py:257
  93.5 14.6 %all-to-all-start.1 = ((f16[16,4,32,128]{3,2,1,0:T(8,128)(2,1)}), f16[16,4,32,128]{3,2,1,0:T(8,128)(2,1)S(1)}, u32[]{:S(2)}, u32[]{:S(2)}) async-start(f16[16,4,32,128]{3,2,1,0:T(8,128)(2,1)} %bitcast.23), calls=%async_computation.1 | async-start | bytes 1048576 | tf_op jit(solution)/shard_map/all_to_all | solution.py:265
where the time goes:
time: 113 us; the launch traced here: 111 us
  starting transfers between devices  32.6 us (29%)
  waiting for transfers between devices  28.3 us (25%)
  blocking collectives  27.1 us (24%)
  Pallas kernels  13.3 us (12%)
  local copies, waits for them, and re-layouts  4.61 us (4%)
  other arithmetic  3.57 us (3%)
    all_gather x1, blocking collectives, balanced(): lax.all_gather(packed, ('tile', 'ka'), axis=0, tiled=False).astype(BF16)  27.1 us
    ppermute x5, waiting for transfers between devices, local(): lax.ppermute(value, 'tile', [(i, (i + by) % chips) for i in range(chips)])  11.8 us
    ppermute x5, starting transfers between devices, local(): lax.ppermute(value, 'tile', [(i, (i + by) % chips) for i in range(chips)])  10.5 us
    all_to_all x1, waiting for transfers between devices, local(): lax.all_to_all(outgoing, 'frag', split_axis=0, concat_axis=0, tiled=True)  8.76 us
    all_to_all x1, starting transfers between devices, local(): lax.all_to_all(outgoing, 'frag', split_axis=0, concat_axis=0, tiled=True)  7.49 us
    pallas_call x1, Pallas kernels, balanced(): pl.pallas_call(fock_body, out_shape=(half, half), in_specs=[SMEM] * 3 + [...  6.98 us
    all_to_all x1, starting transfers between devices, local(): lax.all_to_all(summed, 'frag', split_axis=0, concat_axis=0, tiled=True)  6.24 us
    ppermute x1, starting transfers between devices, balanced(): lax.ppermute(slab_rows, 'frag', [(i + 1, i) for i in range(groups - 1)])  6.03 us
  transfers between devices with their start and end apart: 10, of which 6 were waited for; matrix products, arithmetic and copies ran while one was open for 3% of the time, Pallas kernels for 3%

commit v1 on v0

--- a/solution.py
+++ b/solution.py
@@ -16,6 +16,7 @@
 CLASSES = (16, 19, 32)
 PAIR_SCALE = 0.25
 SUM_SCALE = 0.03125
+SMALL_GRANT = 8 << 20
 SMEM = pl.BlockSpec(memory_space=pltpu.SMEM)
 VMEM = pl.BlockSpec(memory_space=pltpu.VMEM)
 
@@ -35,19 +36,30 @@
     return jnp.where((rows < size) & (cols < size), value, jnp.zeros_like(value))
 
 
-def send_body(where, sizes, slots, density, out, kind, pack, back, targets):
+def send_body(where, sizes, slots, density, out, targets):
     per_group, slab, width = density.shape
-    groups = out.shape[0]
+    first = where[0] * per_group
+    for slot in range(slots.shape[0]):
+        local = slots[slot] - first
+        inside = (local >= 0) & (local < per_group)
+        targets[jnp.where(inside, local, per_group)] = slot // per_group
+    for j in range(per_group):
+        rows = masked_rows(
+            density[j].astype(F32), sizes[first + j], where[1] * slab, 0
+        ).astype(BF16)
+        for c in range(width // TILE):
+            out[targets[j], c] = rows[:, c * TILE : (c + 1) * TILE]
+
+
+def tables_body(where, sizes, slots, kind, pack, back):
+    groups = back.shape[0] // TILES
+    per_group = slots.shape[0] // groups
     first = where[0] * per_group
     widest = jnp.int32(0)
     for group in range(groups):
         total = jnp.int32(0)
         for k in range(per_group):
-            frag = slots[group * per_group + k]
-            total = total + tiles_of(sizes[frag])
-            local = frag - first
-            inside = (local >= 0) & (local < per_group)
-            targets[jnp.where(inside, local, per_group)] = group
+            total = total + held_slot(sizes, slots, group * per_group, k)[1]
         widest = jnp.maximum(widest, total)
     index = jnp.int32(0)
     for limit in CLASSES[:-1]:
@@ -66,12 +78,6 @@
             pack[jnp.where(valid, offset + c, pack.shape[0] - 1)] = source * TILES + c
             back[source * TILES + c] = jnp.where(valid, offset + c, 0)
         offset = offset + count
-    for j in range(per_group):
-        rows = masked_rows(
-            density[j].astype(F32), sizes[first + j], where[1] * slab, 0
-        ).astype(BF16)
-        for c in range(width // TILE):
-            out[targets[j], c] = rows[:, c * TILE : (c + 1) * TILE]
 
 
 def fock_body(
@@ -206,20 +212,25 @@
 
     block = (groups, TILES, slab, TILE)
     table = lambda count: jax.ShapeDtypeStruct((count,), jnp.int32)
-    outgoing, kind, pack, back, targets = pl.pallas_call(
+    outgoing, targets = pl.pallas_call(
         send_body,
-        out_shape=(
-            jax.ShapeDtypeStruct(block, BF16),
-            table(1),
-            table(per_group * TILES + 1),
-            table(groups * TILES),
-            table(per_group + 1),
-        ),
+        out_shape=(jax.ShapeDtypeStruct(block, BF16), table(per_group + 1)),
         in_specs=[SMEM, SMEM, SMEM, VMEM],
-        out_specs=(VMEM, SMEM, SMEM, SMEM, SMEM),
+        out_specs=(VMEM, SMEM),
+        compiler_params=pltpu.CompilerParams(vmem_limit_bytes=SMALL_GRANT),
         name="send",
     )(where, sizes, slot_fragment, density)
     received = lax.all_to_all(outgoing, "frag", split_axis=0, concat_axis=0, tiled=True)
+    low = lax.ppermute(density, "frag", [(i, i + 1) for i in range(groups - 1)])
+    high = lax.ppermute(density, "frag", [(i + 1, i) for i in range(groups - 1)])
+    kind, pack, back = pl.pallas_call(
+        tables_body,
+        out_shape=(table(1), table(per_group * TILES + 1), table(groups * TILES)),
+        in_specs=[SMEM] * 3,
+        out_specs=(SMEM, SMEM, SMEM),
+        name="tables",
+    )(where, sizes, slot_fragment)
+    received, low, high = lax.optimization_barrier((received, low, high))
 
     def balanced(capacity, received):
         split = (capacity + 1) // 2
@@ -245,22 +256,22 @@
             ),
             name="fock",
         )(where, sizes, slot_fragment, gathered, integrals)
-        other = lax.ppermute(send, "ka", [(0, 1), (1, 0)])
-        pair = (keep + other) * PAIR_SCALE
-        up = shift(pair[half_chips:, :split].astype(F16), 1)
-        down = shift(pair[half_chips:, split:].astype(F16), -1)
-        own = pair[:half_chips] + jnp.concatenate([up, down], axis=1).astype(F32)
-        far = own.astype(F16)
-        slab_rows, far = lax.optimization_barrier((density, far))
-        moved = [shift(far[step], 2 * step) for step in range(1, half_chips)]
-        low = lax.ppermute(slab_rows, "frag", [(i, i + 1) for i in range(groups - 1)])
-        high = lax.ppermute(slab_rows, "frag", [(i + 1, i) for i in range(groups - 1)])
+        narrow = lambda value: (value * PAIR_SCALE).astype(F16)
+        across = lambda value: lax.ppermute(value, "ka", [(0, 1), (1, 0)])
+        far = slice(half_chips, chips)
+        opposite = (keep[far] * PAIR_SCALE + across(narrow(send[far])).astype(F32)).astype(F16)
+        up = shift(opposite[:, :split], 1)
+        down = shift(opposite[:, split:], -1)
+        near = slice(0, half_chips)
+        pair = keep[near] * PAIR_SCALE + across(narrow(send[near])).astype(F32)
+        own = pair + jnp.concatenate([up, down], axis=1).astype(F32)
+        moved = [shift(own[step].astype(F16), 2 * step) for step in range(1, half_chips)]
         total = own[0] + sum(part.astype(F32) for part in moved)
         total = lax.optimization_barrier((total * (SUM_SCALE / PAIR_SCALE)).astype(F16))
-        return jnp.take(total, back, axis=0, mode="clip"), low, high
+        return jnp.take(total, back, axis=0, mode="clip")
 
     branches = [functools.partial(balanced, capacity) for capacity in CLASSES]
-    summed, low, high = lax.switch(kind[0], branches, received)
+    summed = lax.switch(kind[0], branches, received)
     summed = summed.reshape(block)
     returned = lax.all_to_all(summed, "frag", split_axis=0, concat_axis=0, tiled=True)
     base = pl.pallas_call(
@@ -268,6 +279,7 @@
         out_shape=jax.ShapeDtypeStruct(density.shape, F32),
         in_specs=[SMEM] * 3 + [VMEM] * 5,
         out_specs=VMEM,
+        compiler_params=pltpu.CompilerParams(vmem_limit_bytes=SMALL_GRANT),
         name="base",
     )(where, sizes, neighbors, low, density, high, hcore, couple)
     picked = jnp.take(returned, targets[:per_group], axis=0, mode="clip")

time: 113 us -> 115 us (1.018)
  the two profiles are of different devices: /device:TPU:2 before, /device:TPU:32 now
where the time goes in v1:
time: 115 us
  waiting for transfers between devices  39.8 us (35%)
  starting transfers between devices  28.6 us (25%)
  blocking collectives  25.8 us (22%)
  Pallas kernels  11.6 us (10%)
  local copies, waits for them, and re-layouts  4.99 us (4%)
  other arithmetic  2.53 us (2%)
    all_gather x1, blocking collectives, balanced(): lax.all_gather(packed, ('tile', 'ka'), axis=0, tiled=False).astype(BF16)  25.8 us
    ppermute x5, waiting for transfers between devices, local(): lax.ppermute(value, 'tile', [(i, (i + by) % chips) for i in range(chips)])  22.5 us
    ppermute x5, starting transfers between devices, local(): lax.ppermute(value, 'tile', [(i, (i + by) % chips) for i in range(chips)])  9.42 us
    all_to_all x1, waiting for transfers between devices, local(): lax.all_to_all(summed, 'frag', split_axis=0, concat_axis=0, tiled=True)  9.02 us
    all_to_all x1, starting transfers between devices, local(): lax.all_to_all(outgoing, 'frag', split_axis=0, concat_axis=0, tiled=True)  7.05 us
    all_to_all x1, starting transfers between devices, local(): lax.all_to_all(summed, 'frag', split_axis=0, concat_axis=0, tiled=True)  6.41 us
    pallas_call x1, Pallas kernels, balanced(): pl.pallas_call(fock_body, out_shape=(half, half), in_specs=[SMEM] * 3 + [...  5.83 us
    ppermute x1, waiting for transfers between devices, local(): low = lax.ppermute(density, 'frag', [(i, i + 1) for i in range(groups - 1)])  4.37 us
  transfers between devices with their start and end apart: 11, of which 8 were waited for; matrix products, arithmetic and copies ran while one was open for 1% of the time, Pallas kernels for 3%

profile of v1, /device:TPU:32, one launch (start us, length us, event | category | flops | bytes accessed | tf_op | source)
XLA Modules:
  0.0 114.8 jit_solution(8401949394286778860)
XLA Ops:
  1.0 1.8 %send.1 = (bf16[16,4,32,128]{3,2,1,0:T(8,128)(2,1)}, s32[9]{0:T(128)S(1)}) custom-call(s32[4]{0:T(128)S(1)} %pad_add_fusion.where, s32[128]{0:T(128)} %sizes.5, s32[128]{0:T(128)} %slots.3, bf16[8,32,512]{2,1,0:T(8,128)(2,1)S(1)} %copy-done), custom_call_target="tpu_custom_call" | custom-call | tf_op jit(solution)/shard_map/send/pallas_call | solution.py:215
  2.9 7.0 %all-to-all-start = ((bf16[16,4,32,128]{3,2,1,0:T(8,128)(2,1)}), bf16[16,4,32,128]{3,2,1,0:T(8,128)(2,1)S(1)}, u32[]{:S(2)}, u32[]{:S(2)}) async-start(bf16[16,4,32,128]{3,2,1,0:T(8,128)(2,1)} %get-tuple-element.86), calls=%async_computation | async-start | bytes 1048576 | tf_op jit(solution)/shard_map/all_to_all | solution.py:223
  9.9 3.8 %collective-permute-start.21 = (bf16[8,32,512]{2,1,0:T(8,128)(2,1)}, bf16[8,32,512]{2,1,0:T(8,128)(2,1)S(1)}, u32[]{:S(2)}, u32[]{:S(2)}) collective-permute-start(bf16[8,32,512]{2,1,0:T(8,128)(2,1)} %own.1), channel_id=1, source_target_pairs={{0,16},{16,32},{32,48},{48,64},{64,80},{80,96},{96,112},{112,128},... | collective-permute-start | bytes 786440 | tf_op jit(solution)/shard_map/ppermute | solution.py:224
  13.8 1.3 %collective-permute-start.22 = (bf16[8,32,512]{2,1,0:T(8,128)(2,1)}, bf16[8,32,512]{2,1,0:T(8,128)(2,1)S(1)}, u32[]{:S(2)}, u32[]{:S(2)}) collective-permute-start(bf16[8,32,512]{2,1,0:T(8,128)(2,1)} %own.1), channel_id=1, source_target_pairs={{16,0},{32,16},{48,32},{64,48},{80,64},{96,80},{112,96},{128,112},... | collective-permute-start | bytes 786440 | tf_op jit(solution)/shard_map/ppermute | solution.py:225
  15.1 2.2 %tables.1 = (s32[1]{0:T(128)}, s32[33]{0:T(128)S(1)}, s32[64]{0:T(128)S(1)}) custom-call(s32[4]{0:T(128)S(1)} %pad_add_fusion.where, s32[128]{0:T(128)} %sizes.5, s32[128]{0:T(128)} %slots.3), custom_call_target="tpu_custom_call" | custom-call | tf_op jit(solution)/shard_map/tables/pallas_call | solution.py:226
  17.9 4.4 %collective-permute-done.21.low = bf16[8,32,512]{2,1,0:T(8,128)(2,1)S(1)} collective-permute-done((bf16[8,32,512]{2,1,0:T(8,128)(2,1)}, bf16[8,32,512]{2,1,0:T(8,128)(2,1)S(1)}, u32[]{:S(2)}, u32[]{:S(2)}) %collective-permute-start.21) | collective-permute-done | bytes 262176 | tf_op jit(solution)/shard_map/ppermute | solution.py:224
  22.3 2.4 %collective-permute-done.22.high = bf16[8,32,512]{2,1,0:T(8,128)(2,1)S(1)} collective-permute-done((bf16[8,32,512]{2,1,0:T(8,128)(2,1)}, bf16[8,32,512]{2,1,0:T(8,128)(2,1)S(1)}, u32[]{:S(2)}, u32[]{:S(2)}) %collective-permute-start.22) | collective-permute-done | bytes 262176 | tf_op jit(solution)/shard_map/ppermute | solution.py:225
  24.8 70.3 %conditional.1 = (f16[64,32,128]{2,1,0:T(8,128)(2,1)}) conditional(s32[]{:T(128)} %bitcast.22, (bf16[16,4,32,128]{3,2,1,0:T(8,128)(2,1)S(1)}, s32[33]{0:T(128)S(1)}, s32[4]{0:T(128)S(1)}, s32[128]{0:T(128)}, s32[128]{0:T(128)}, /*index=5*/bf16[8,2,512,512]{3,2,1,0:T(8,128)(2,1)}, s32[64]{0:T(128)S(1)}) %tuple.16, ...), branch_computations={%region_0.1_spmd, %region_1.2_spmd, %region_2.3_spmd} | conditional | flops 11143168 | bytes 87307384 | solution.py:274
  25.5 25.8 %all-gather.7 = f16[304,32,128]{2,1,0:T(8,128)(2,1)S(1)} all-gather(f16[19,32,128]{2,1,0:T(8,128)(2,1)S(1)} %convert_element_type.146), channel_id=3, replica_groups=mesh['frag'=16,'tile'=8,'ka'=2] {'tile','ka'}, dimensions={0}, use_global_device_ids=true | all-gather | bytes 2646016 | tf_op jit(solution)/shard_map/cond/branch_1_fun/all_gather | solution.py:240
  52.0 5.8 %fock.4 = (f32[8,19,32,128]{3,2,1,0:T(8,128)S(1)}, f32[8,19,32,128]{3,2,1,0:T(8,128)S(1)}) custom-call(s32[4]{0:T(128)S(1)} %get-tuple-element.60.where, s32[128]{0:T(128)S(1)} %copy-done.7, s32[128]{0:T(128)S(1)} %copy-done.10, bf16[16,19,32,128]{3,2,1,0:T(8,128)(2,1)S(1)} %bitcast.67, bf16[8,2,512,512]{3,2,1,0:T(8,128)(2,1)} %get-tuple-element.65.factors), custom_call_target="tpu_custom_call" | custom-call | tf_op jit(solution)/shard_map/cond/branch_1_fun/fock/pallas_call | solution.py:242
  58.7 1.5 %collective-permute-done.1 = f16[4,19,32,128]{3,2,1,0:T(8,128)(2,1)S(1)} collective-permute-done((f16[4,19,32,128]{3,2,1,0:T(8,128)(2,1)S(1)}, f16[4,19,32,128]{3,2,1,0:T(8,128)(2,1)S(1)}, u32[]{:S(2)}, u32[]{:S(2)}) %collective-permute-start.1) | collective-permute-done | bytes 622624 | tf_op jit(solution)/shard_map/cond/branch_1_fun/ppermute | solution.py:260
  60.6 1.0 collective-permute-start.2
  61.6 1.2 %collective-permute-start.3 = (f16[4,9,32,128]{3,2,1,0:T(8,128)(2,1)S(1)}, f16[4,9,32,128]{3,2,1,0:T(8,128)(2,1)S(1)}, u32[]{:S(2)}, u32[]{:S(2)}) collective-permute-start(f16[4,9,32,128]{3,2,1,0:T(8,128)(2,1)S(1)} %slice.133), channel_id=1, source_target_pairs={{0,14},{2,0},{4,2},{6,4},{8,6},{10,8},{12,10},{14,12},{1,15},{3,1}... | collective-permute-start | bytes 884744 | tf_op jit(solution)/shard_map/cond/branch_1_fun/ppermute | solution.py:209
  62.8 7.9 %collective-permute-done.3 = f16[4,9,32,128]{3,2,1,0:T(8,128)(2,1)S(1)} collective-permute-done((f16[4,9,32,128]{3,2,1,0:T(8,128)(2,1)S(1)}, f16[4,9,32,128]{3,2,1,0:T(8,128)(2,1)S(1)}, u32[]{:S(2)}, u32[]{:S(2)}) %collective-permute-start.3) | collective-permute-done | bytes 294944 | tf_op jit(solution)/shard_map/cond/branch_1_fun/ppermute | solution.py:209
  71.2 4.6 %collective-permute-start.6 = (f16[19,32,128]{2,1,0:T(8,128)(2,1)S(1)}, f16[19,32,128]{2,1,0:T(8,128)(2,1)S(1)}, u32[]{:S(2)}, u32[]{:S(2)}) collective-permute-start(f16[19,32,128]{2,1,0:T(8,128)(2,1)S(1)} %get-tuple-element.110), channel_id=1, source_target_pairs={{0,12},{2,14},{4,0},{6,2},{8,4},{10,6},{12,8},{14,10},{1,13},{3,15... | collective-permute-start | bytes 466952 | tf_op jit(solution)/shard_map/cond/branch_1_fun/ppermute | solution.py:209
  75.7 2.7 %collective-permute-start.5 = (f16[19,32,128]{2,1,0:T(8,128)(2,1)S(1)}, f16[19,32,128]{2,1,0:T(8,128)(2,1)S(1)}, u32[]{:S(2)}, u32[]{:S(2)}) collective-permute-start(f16[19,32,128]{2,1,0:T(8,128)(2,1)S(1)} %get-tuple-element.111), channel_id=1, source_target_pairs={{0,8},{2,10},{4,12},{6,14},{8,0},{10,2},{12,4},{14,6},{1,9},{3,11}... | collective-permute-start | bytes 466952 | tf_op jit(solution)/shard_map/cond/branch_1_fun/ppermute | solution.py:209
  78.4 6.9 %collective-permute-done.6 = f16[19,32,128]{2,1,0:T(8,128)(2,1)S(1)} collective-permute-done((f16[19,32,128]{2,1,0:T(8,128)(2,1)S(1)}, f16[19,32,128]{2,1,0:T(8,128)(2,1)S(1)}, u32[]{:S(2)}, u32[]{:S(2)}) %collective-permute-start.6) | collective-permute-done | bytes 155680 | tf_op jit(solution)/shard_map/cond/branch_1_fun/ppermute | solution.py:209
  85.3 6.1 %collective-permute-done.5 = f16[19,32,128]{2,1,0:T(8,128)(2,1)S(1)} collective-permute-done((f16[19,32,128]{2,1,0:T(8,128)(2,1)S(1)}, f16[19,32,128]{2,1,0:T(8,128)(2,1)S(1)}, u32[]{:S(2)}, u32[]{:S(2)}) %collective-permute-start.5) | collective-permute-done | bytes 155680 | tf_op jit(solution)/shard_map/cond/branch_1_fun/ppermute | solution.py:209
  91.4 1.6 %collective-permute-done.4 = f16[19,32,128]{2,1,0:T(8,128)(2,1)S(1)} collective-permute-done((f16[19,32,128]{2,1,0:T(8,128)(2,1)S(1)}, f16[19,32,128]{2,1,0:T(8,128)(2,1)S(1)}, u32[]{:S(2)}, u32[]{:S(2)}) %collective-permute-start.4) | collective-permute-done | bytes 155680 | tf_op jit(solution)/shard_map/cond/branch_1_fun/ppermute | solution.py:209
  93.1 1.5 %gather_fusion.1 = f16[64,32,128]{2,1,0:T(8,128)(2,1)} fusion(f16[19,32,128]{2,1,0:T(8,128)(2,1)S(1)} %fusion.5, s32[1024]{0:T(1024)S(1)} %pad_clamp_fusion.2), kind=kCustom, calls=%fused_computation.3 | custom fusion | bytes 1048832 | tf_op jit(solution)/shard_map/cond/branch_1_fun/jit(_take)/gather | solution.py:271
  95.1 6.4 %all-to-all-start.1 = ((f16[16,4,32,128]{3,2,1,0:T(8,128)(2,1)}), f16[16,4,32,128]{3,2,1,0:T(8,128)(2,1)S(1)}, u32[]{:S(2)}, u32[]{:S(2)}) async-start(f16[16,4,32,128]{3,2,1,0:T(8,128)(2,1)} %bitcast.23), calls=%async_computation.1 | async-start | bytes 1048576 | tf_op jit(solution)/shard_map/all_to_all | solution.py:276
  102.4 1.8 %base.1 = f32[8,32,512]{2,1,0:T(8,128)S(1)} custom-call(s32[4]{0:T(128)S(1)} %pad_add_fusion.where, s32[128]{0:T(128)S(1)} %copy-done.5, s32[8,4]{1,0:T(8,128)S(1)} %copy.11.neighbors, bf16[8,32,512]{2,1,0:T(8,128)(2,1)S(1)} %collective-permute-done.21.low, bf16[8,32,512]{2,1,0:T(8,128)(2,1)S(1)} %copy-done.1, ...), custom_call_target="tpu_custom_call" | custom-call | tf_op jit(solution)/shard_map/base/pallas_call | solution.py:277
  104.2 9.0 %all-to-all-done.1 = f16[16,4,32,128]{3,2,1,0:T(8,128)(2,1)S(1)} async-done(((f16[16,4,32,128]{3,2,1,0:T(8,128)(2,1)}), f16[16,4,32,128]{3,2,1,0:T(8,128)(2,1)S(1)}, u32[]{:S(2)}, u32[]{:S(2)}) %all-to-all-start.1) | async-done | bytes 524320 | tf_op jit(solution)/shard_map/all_to_all | solution.py:276
  113.8 1.0 fusion.9
  (40 shorter events, 5.7 us)
Async XLA Ops:
  0.1 1.0 copy-start
  2.9 21.9 %all-to-all-start = ((bf16[16,4,32,128]{3,2,1,0:T(8,128)(2,1)}), bf16[16,4,32,128]{3,2,1,0:T(8,128)(2,1)S(1)}, u32[]{:S(2)}, u32[]{:S(2)}) async-start(bf16[16,4,32,128]{3,2,1,0:T(8,128)(2,1)} %get-tuple-element.86), calls=%async_computation | async-start | bytes 1048576 | tf_op jit(solution)/shard_map/all_to_all | solution.py:223
  9.9 12.4 %collective-permute-start.21 = (bf16[8,32,512]{2,1,0:T(8,128)(2,1)}, bf16[8,32,512]{2,1,0:T(8,128)(2,1)S(1)}, u32[]{:S(2)}, u32[]{:S(2)}) collective-permute-start(bf16[8,32,512]{2,1,0:T(8,128)(2,1)} %own.1), channel_id=1, source_target_pairs={{0,16},{16,32},{32,48},{48,64},{64,80},{80,96},{96,112},{112,128},... | collective-permute-start | bytes 786440 | tf_op jit(solution)/shard_map/ppermute | solution.py:224
  13.8 11.0 %collective-permute-start.22 = (bf16[8,32,512]{2,1,0:T(8,128)(2,1)}, bf16[8,32,512]{2,1,0:T(8,128)(2,1)S(1)}, u32[]{:S(2)}, u32[]{:S(2)}) collective-permute-start(bf16[8,32,512]{2,1,0:T(8,128)(2,1)} %own.1), channel_id=1, source_target_pairs={{16,0},{32,16},{48,32},{64,48},{80,64},{96,80},{112,96},{128,112},... | collective-permute-start | bytes 786440 | tf_op jit(solution)/shard_map/ppermute | solution.py:225
  24.8 76.8 %copy-start.12 = (s32[8,4]{0,1:T(4,128)S(1)}, s32[8,4]{0,1:T(4,128)}, u32[]{:S(2)}) copy-start(s32[8,4]{0,1:T(4,128)} %param.11) | copy-start | bytes 388
  24.8 77.6 %copy-start.1 = (bf16[8,32,512]{2,1,0:T(8,128)(2,1)S(1)}, bf16[8,32,512]{2,1,0:T(8,128)(2,1)}, u32[]{:S(2)}) copy-start(bf16[8,32,512]{2,1,0:T(8,128)(2,1)} %own.1) | copy-start | bytes 786436
  24.8 77.6 %copy-start.2 = (bf16[8,4,32,512]{3,2,1,0:T(8,128)(2,1)S(1)}, bf16[8,4,32,512]{3,2,1,0:T(8,128)(2,1)}, u32[]{:S(2)}) copy-start(bf16[8,4,32,512]{3,2,1,0:T(8,128)(2,1)} %couple.1) | copy-start | bytes 3145732
  24.8 77.6 %copy-start.3 = (bf16[8,32,512]{2,1,0:T(8,128)(2,1)S(1)}, bf16[8,32,512]{2,1,0:T(8,128)(2,1)}, u32[]{:S(2)}) copy-start(bf16[8,32,512]{2,1,0:T(8,128)(2,1)} %hcore.1) | copy-start | bytes 786436
  24.8 77.6 %copy-start.5 = (s32[128]{0:T(128)S(1)}, s32[128]{0:T(128)}, u32[]{:S(2)}) copy-start(s32[128]{0:T(128)} %sizes.5) | copy-start | bytes 1540
  51.3 0.7 copy-start.7
  51.3 0.7 copy-start.10
  58.1 2.1 %collective-permute-start.1 = (f16[4,19,32,128]{3,2,1,0:T(8,128)(2,1)S(1)}, f16[4,19,32,128]{3,2,1,0:T(8,128)(2,1)S(1)}, u32[]{:S(2)}, u32[]{:S(2)}) collective-permute-start(f16[4,19,32,128]{3,2,1,0:T(8,128)(2,1)S(1)} %get-tuple-element.108), channel_id=1, source_target_pairs={{0,1},{1,0},{2,3},{3,2},{4,5},{5,4},{6,7},{7,6},{8,9},{9,8},{10,11... | collective-permute-start | bytes 1867784 | tf_op jit(solution)/shard_map/cond/branch_1_fun/ppermute | solution.py:260
  58.6 4.2 %collective-permute-start = (f16[4,19,32,128]{3,2,1,0:T(8,128)(2,1)S(1)}, f16[4,19,32,128]{3,2,1,0:T(8,128)(2,1)S(1)}, u32[]{:S(2)}, u32[]{:S(2)}) collective-permute-start(f16[4,19,32,128]{3,2,1,0:T(8,128)(2,1)S(1)} %get-tuple-element.107), channel_id=1, source_target_pairs={{0,1},{1,0},{2,3},{3,2},{4,5},{5,4},{6,7},{7,6},{8,9},{9,8},{10,11... | collective-permute-start | bytes 1867784 | tf_op jit(solution)/shard_map/cond/branch_1_fun/ppermute | solution.py:260
  60.6 10.1 %collective-permute-start.2 = (f16[4,10,32,128]{3,2,1,0:T(8,128)(2,1)S(1)}, f16[4,10,32,128]{3,2,1,0:T(8,128)(2,1)S(1)}, u32[]{:S(2)}, u32[]{:S(2)}) collective-permute-start(f16[4,10,32,128]{3,2,1,0:T(8,128)(2,1)S(1)} %slice.132), channel_id=1, source_target_pairs={{0,2},{2,4},{4,6},{6,8},{8,10},{10,12},{12,14},{14,0},{1,3},{3,5},... | collective-permute-start | bytes 983048 | tf_op jit(solution)/shard_map/cond/branch_1_fun/ppermute | solution.py:209
  61.6 9.1 %collective-permute-start.3 = (f16[4,9,32,128]{3,2,1,0:T(8,128)(2,1)S(1)}, f16[4,9,32,128]{3,2,1,0:T(8,128)(2,1)S(1)}, u32[]{:S(2)}, u32[]{:S(2)}) collective-permute-start(f16[4,9,32,128]{3,2,1,0:T(8,128)(2,1)S(1)} %slice.133), channel_id=1, source_target_pairs={{0,14},{2,0},{4,2},{6,4},{8,6},{10,8},{12,10},{14,12},{1,15},{3,1}... | collective-permute-start | bytes 884744 | tf_op jit(solution)/shard_map/cond/branch_1_fun/ppermute | solution.py:209
  71.2 14.1 %collective-permute-start.6 = (f16[19,32,128]{2,1,0:T(8,128)(2,1)S(1)}, f16[19,32,128]{2,1,0:T(8,128)(2,1)S(1)}, u32[]{:S(2)}, u32[]{:S(2)}) collective-permute-start(f16[19,32,128]{2,1,0:T(8,128)(2,1)S(1)} %get-tuple-element.110), channel_id=1, source_target_pairs={{0,12},{2,14},{4,0},{6,2},{8,4},{10,6},{12,8},{14,10},{1,13},{3,15... | collective-permute-start | bytes 466952 | tf_op jit(solution)/shard_map/cond/branch_1_fun/ppermute | solution.py:209
  75.7 15.7 %collective-permute-start.5 = (f16[19,32,128]{2,1,0:T(8,128)(2,1)S(1)}, f16[19,32,128]{2,1,0:T(8,128)(2,1)S(1)}, u32[]{:S(2)}, u32[]{:S(2)}) collective-permute-start(f16[19,32,128]{2,1,0:T(8,128)(2,1)S(1)} %get-tuple-element.111), channel_id=1, source_target_pairs={{0,8},{2,10},{4,12},{6,14},{8,0},{10,2},{12,4},{14,6},{1,9},{3,11}... | collective-permute-start | bytes 466952 | tf_op jit(solution)/shard_map/cond/branch_1_fun/ppermute | solution.py:209
  78.4 14.6 %collective-permute-start.4 = (f16[19,32,128]{2,1,0:T(8,128)(2,1)S(1)}, f16[19,32,128]{2,1,0:T(8,128)(2,1)S(1)}, u32[]{:S(2)}, u32[]{:S(2)}) collective-permute-start(f16[19,32,128]{2,1,0:T(8,128)(2,1)S(1)} %get-tuple-element.109), channel_id=1, source_target_pairs={{0,4},{2,6},{4,8},{6,10},{8,12},{10,14},{12,0},{14,2},{1,5},{3,7},... | collective-permute-start | bytes 466952 | tf_op jit(solution)/shard_map/cond/branch_1_fun/ppermute | solution.py:209
  95.1 18.1 %all-to-all-start.1 = ((f16[16,4,32,128]{3,2,1,0:T(8,128)(2,1)}), f16[16,4,32,128]{3,2,1,0:T(8,128)(2,1)S(1)}, u32[]{:S(2)}, u32[]{:S(2)}) async-start(f16[16,4,32,128]{3,2,1,0:T(8,128)(2,1)} %bitcast.23), calls=%async_computation.1 | async-start | bytes 1048576 | tf_op jit(solution)/shard_map/all_to_all | solution.py:276

commit v2 on v1

--- a/solution.py
+++ b/solution.py
@@ -13,7 +13,7 @@
 BF16 = jnp.bfloat16
 TILE = 128
 TILES = 4
-CLASSES = (16, 19, 32)
+CLASSES = (17, 21, 32)
 PAIR_SCALE = 0.25
 SUM_SCALE = 0.03125
 SMALL_GRANT = 8 << 20
@@ -108,11 +108,23 @@
 
     def run(k, offset, tiles):
         extent = tiles * TILE
-        pieces = [(r, c) for r in range(extent // slab) for c in range(tiles)]
-        rows = lambda r: slice(r * slab, (r + 1) * slab)
+        bands = extent // slab
+        rows = lambda r: pl.ds(r * slab, slab)
         cols = lambda c: slice(c * TILE, (c + 1) * TILE)
-        for r, c in pieces:
-            dense[rows(r), cols(c)] = gathered[r, offset + c]
+
+        def each(count, step, carry):
+            if tiles == TILES:
+                return lax.fori_loop(0, count, step, carry)
+            for index in range(count):
+                carry = step(index, carry)
+            return carry
+
+        def unpack(r, carry):
+            for c in range(tiles):
+                dense[rows(r), cols(c)] = gathered[r, offset + c]
+            return carry
+
+        each(bands, unpack, 0)
         for copy in copies(k, tiles):
             copy.wait()
         block = dense[:extent, :extent]
@@ -128,10 +140,14 @@
             preferred_element_type=F32,
         )
         factor = lambda q, r, c: vectors[k, rows(r), cols(q * tiles + c)].astype(F32)
-        sums = [jnp.zeros((slab, TILE), F32) for _ in range(chol)]
-        for r, c in pieces:
-            part = dense[rows(r), cols(c)].astype(F32)
-            sums = [value + factor(q, r, c) * part for q, value in enumerate(sums)]
+
+        def weigh(r, sums):
+            for c in range(tiles):
+                part = dense[rows(r), cols(c)].astype(F32)
+                sums = [value + factor(q, r, c) * part for q, value in enumerate(sums)]
+            return sums
+
+        sums = each(bands, weigh, [jnp.zeros((slab, TILE), F32) for _ in range(chol)])
         coulomb = [jnp.sum(value, keepdims=True) for value in sums]
 
         def finish(r, c):
@@ -141,7 +157,8 @@
             return value
 
         first_core = mine == 0
-        for target in range(extent // (2 * slab)):
+
+        def store(target, carry):
             same = (target + chip) % 2 == 0
             own_row = (target // 2 + half - chip // 2) % half
             up_row = half + (target // 2 + half - right // 2) % half
@@ -154,6 +171,9 @@
                 odd = finish(2 * target + 1, c)
                 keep[row, place] = jnp.where(first_core, even, odd)
                 send[row, place] = jnp.where(first_core, odd, even)
+            return carry
+
+        each(bands // 2, store, 0)
 
     for k in range(per_group):
         _, count = held_slot(sizes, slots, first, k)
@@ -221,8 +241,6 @@
         name="send",
     )(where, sizes, slot_fragment, density)
     received = lax.all_to_all(outgoing, "frag", split_axis=0, concat_axis=0, tiled=True)
-    low = lax.ppermute(density, "frag", [(i, i + 1) for i in range(groups - 1)])
-    high = lax.ppermute(density, "frag", [(i + 1, i) for i in range(groups - 1)])
     kind, pack, back = pl.pallas_call(
         tables_body,
         out_shape=(table(1), table(per_group * TILES + 1), table(groups * TILES)),
@@ -230,7 +248,6 @@
         out_specs=(SMEM, SMEM, SMEM),
         name="tables",
     )(where, sizes, slot_fragment)
-    received, low, high = lax.optimization_barrier((received, low, high))
 
     def balanced(capacity, received):
         split = (capacity + 1) // 2
@@ -262,16 +279,18 @@
         opposite = (keep[far] * PAIR_SCALE + across(narrow(send[far])).astype(F32)).astype(F16)
         up = shift(opposite[:, :split], 1)
         down = shift(opposite[:, split:], -1)
+        low = lax.ppermute(density, "frag", [(i, i + 1) for i in range(groups - 1)])
+        high = lax.ppermute(density, "frag", [(i + 1, i) for i in range(groups - 1)])
         near = slice(0, half_chips)
         pair = keep[near] * PAIR_SCALE + across(narrow(send[near])).astype(F32)
         own = pair + jnp.concatenate([up, down], axis=1).astype(F32)
         moved = [shift(own[step].astype(F16), 2 * step) for step in range(1, half_chips)]
         total = own[0] + sum(part.astype(F32) for part in moved)
         total = lax.optimization_barrier((total * (SUM_SCALE / PAIR_SCALE)).astype(F16))
-        return jnp.take(total, back, axis=0, mode="clip")
+        return jnp.take(total, back, axis=0, mode="clip"), low, high
 
     branches = [functools.partial(balanced, capacity) for capacity in CLASSES]
-    summed = lax.switch(kind[0], branches, received)
+    summed, low, high = lax.switch(kind[0], branches, received)
     summed = summed.reshape(block)
     returned = lax.all_to_all(summed, "frag", split_axis=0, concat_axis=0, tiled=True)
     base = pl.pallas_call(

time: 115 us -> 105 us (0.913)
  the two profiles are of different devices: /device:TPU:32 before, /device:TPU:2 now
where the time goes in v2:
time: 105 us; the launch traced here: 103 us
  starting transfers between devices  33.8 us (32%)
  blocking collectives  26.1 us (25%)
  waiting for transfers between devices  22.4 us (21%)
  Pallas kernels  13.8 us (13%)
  local copies, waits for them, and re-layouts  4.06 us (4%)
  other arithmetic  2.37 us (2%)
    all_gather x1, blocking collectives, balanced(): lax.all_gather(packed, ('tile', 'ka'), axis=0, tiled=False).astype(BF16)  26.1 us
    ppermute x5, starting transfers between devices, local(): lax.ppermute(value, 'tile', [(i, (i + by) % chips) for i in range(chips)])  10.3 us
    ppermute x5, waiting for transfers between devices, local(): lax.ppermute(value, 'tile', [(i, (i + by) % chips) for i in range(chips)])  9.8 us
    all_to_all x1, starting transfers between devices, local(): lax.all_to_all(outgoing, 'frag', split_axis=0, concat_axis=0, tiled=True)  7.49 us
    all_to_all x1, starting transfers between devices, local(): lax.all_to_all(summed, 'frag', split_axis=0, concat_axis=0, tiled=True)  7.45 us
    pallas_call x1, Pallas kernels, balanced(): pl.pallas_call(fock_body, out_shape=(half, half), in_specs=[SMEM] * 3 + [...  7.18 us
    all_to_all x1, waiting for transfers between devices, local(): lax.all_to_all(outgoing, 'frag', split_axis=0, concat_axis=0, tiled=True)  6.45 us
    ppermute x1, starting transfers between devices, balanced(): lax.ppermute(density, 'frag', [(i + 1, i) for i in range(groups - 1)])  6.03 us
  transfers between devices with their start and end apart: 11, of which 6 were waited for; matrix products, arithmetic and copies ran while one was open for 3% of the time, Pallas kernels for 4%

profile of v2, /device:TPU:2, one launch (start us, length us, event | category | flops | bytes accessed | tf_op | source)
XLA Modules:
  0.0 103.5 jit_solution(8106889642532712733)
XLA Ops:
  0.1 2.1 %send.1 = (bf16[16,4,32,128]{3,2,1,0:T(8,128)(2,1)}, s32[9]{0:T(128)S(1)}) custom-call(s32[4]{0:T(128)S(1)} %pad_add_fusion.where, s32[128]{0:T(128)} %sizes.5, s32[128]{0:T(128)} %slots.3, bf16[8,32,512]{2,1,0:T(8,128)(2,1)} %own.1), custom_call_target="tpu_custom_call" | custom-call | tf_op jit(solution)/shard_map/send/pallas_call | solution.py:235
  2.2 7.5 %all-to-all-start = ((bf16[16,4,32,128]{3,2,1,0:T(8,128)(2,1)}), bf16[16,4,32,128]{3,2,1,0:T(8,128)(2,1)S(1)}, u32[]{:S(2)}, u32[]{:S(2)}) async-start(bf16[16,4,32,128]{3,2,1,0:T(8,128)(2,1)} %get-tuple-element.92), calls=%async_computation | async-start | bytes 1048576 | tf_op jit(solution)/shard_map/all_to_all | solution.py:243
  9.7 2.2 %tables.1 = (s32[1]{0:T(128)}, s32[33]{0:T(128)S(1)}, s32[64]{0:T(128)S(1)}) custom-call(s32[4]{0:T(128)S(1)} %pad_add_fusion.where, s32[128]{0:T(128)} %sizes.5, s32[128]{0:T(128)} %slots.3), custom_call_target="tpu_custom_call" | custom-call | tf_op jit(solution)/shard_map/tables/pallas_call | solution.py:244
  12.6 6.4 %all-to-all-done = bf16[16,4,32,128]{3,2,1,0:T(8,128)(2,1)S(1)} async-done(((bf16[16,4,32,128]{3,2,1,0:T(8,128)(2,1)}), bf16[16,4,32,128]{3,2,1,0:T(8,128)(2,1)S(1)}, u32[]{:S(2)}, u32[]{:S(2)}) %all-to-all-start) | async-done | bytes 524320 | tf_op jit(solution)/shard_map/all_to_all | solution.py:243
  19.0 67.5 %conditional.1 = (f16[64,32,128]{2,1,0:T(8,128)(2,1)}, bf16[8,32,512]{2,1,0:T(8,128)(2,1)}, bf16[8,32,512]{2,1,0:T(8,128)(2,1)}) conditional(s32[]{:T(128)} %bitcast.22, (bf16[16,4,32,128]{3,2,1,0:T(8,128)(2,1)S(1)}, s32[33]{0:T(128)S(1)}, s32[4]{0:T(128)S(1)}, s32[128]{0:T(128)}, s32[128]{0:T(128)}, ...), branch_computations={%region_0.1_spmd, %region_1.2_spmd, %region_2.3_spmd} | conditional | flops 11143168 | bytes 90453232 | solution.py:293
  19.7 26.1 %all-gather.6 = f16[272,32,128]{2,1,0:T(8,128)(2,1)S(1)} all-gather(f16[17,32,128]{2,1,0:T(8,128)(2,1)S(1)} %convert_element_type.130), channel_id=2, replica_groups=mesh['frag'=16,'tile'=8,'ka'=2] {'tile','ka'}, dimensions={0}, use_global_device_ids=true | all-gather | bytes 2367488 | tf_op jit(solution)/shard_map/cond/branch_0_fun/all_gather | solution.py:257
  46.5 7.2 %fock.3 = (f32[8,17,32,128]{3,2,1,0:T(8,128)S(1)}, f32[8,17,32,128]{3,2,1,0:T(8,128)S(1)}) custom-call(s32[4]{0:T(128)S(1)} %get-tuple-element.53.where, s32[128]{0:T(128)S(1)} %copy-done.8, s32[128]{0:T(128)S(1)} %copy-done.11, bf16[16,17,32,128]{3,2,1,0:T(8,128)(2,1)S(1)} %bitcast.68, bf16[8,2,512,512]{3,2,1,0:T(8,128)(2,1)} %get-tuple-element.58.factors), custom_call_target="tpu_custom_call" | custom-call | tf_op jit(solution)/shard_map/cond/branch_0_fun/fock/pallas_call | solution.py:259
  54.5 1.4 %collective-permute-done.1 = f16[4,17,32,128]{3,2,1,0:T(8,128)(2,1)S(1)} collective-permute-done((f16[4,17,32,128]{3,2,1,0:T(8,128)(2,1)S(1)}, f16[4,17,32,128]{3,2,1,0:T(8,128)(2,1)S(1)}, u32[]{:S(2)}, u32[]{:S(2)}) %collective-permute-start.1) | collective-permute-done | bytes 557088 | tf_op jit(solution)/shard_map/cond/branch_0_fun/ppermute | solution.py:277
  56.3 0.9 collective-permute-start.2
  57.2 2.5 %collective-permute-start.3 = (f16[4,8,32,128]{3,2,1,0:T(8,128)(2,1)S(1)}, f16[4,8,32,128]{3,2,1,0:T(8,128)(2,1)S(1)}, u32[]{:S(2)}, u32[]{:S(2)}) collective-permute-start(f16[4,8,32,128]{3,2,1,0:T(8,128)(2,1)S(1)} %slice.127), channel_id=1, source_target_pairs={{0,14},{2,0},{4,2},{6,4},{8,6},{10,8},{12,10},{14,12},{1,15},{3,1}... | collective-permute-start | bytes 786440 | tf_op jit(solution)/shard_map/cond/branch_0_fun/ppermute | solution.py:229
  59.7 5.9 %collective-permute-done.3 = f16[4,8,32,128]{3,2,1,0:T(8,128)(2,1)S(1)} collective-permute-done((f16[4,8,32,128]{3,2,1,0:T(8,128)(2,1)S(1)}, f16[4,8,32,128]{3,2,1,0:T(8,128)(2,1)S(1)}, u32[]{:S(2)}, u32[]{:S(2)}) %collective-permute-start.3) | collective-permute-done | bytes 262176 | tf_op jit(solution)/shard_map/cond/branch_0_fun/ppermute | solution.py:229
  65.6 1.2 %collective-permute-done.2 = f16[4,9,32,128]{3,2,1,0:T(8,128)(2,1)S(1)} collective-permute-done((f16[4,9,32,128]{3,2,1,0:T(8,128)(2,1)S(1)}, f16[4,9,32,128]{3,2,1,0:T(8,128)(2,1)S(1)}, u32[]{:S(2)}, u32[]{:S(2)}) %collective-permute-start.2) | collective-permute-done | bytes 294944 | tf_op jit(solution)/shard_map/cond/branch_0_fun/ppermute | solution.py:229
  67.4 3.2 %collective-permute-start.5 = (f16[17,32,128]{2,1,0:T(8,128)(2,1)S(1)}, f16[17,32,128]{2,1,0:T(8,128)(2,1)S(1)}, u32[]{:S(2)}, u32[]{:S(2)}) collective-permute-start(f16[17,32,128]{2,1,0:T(8,128)(2,1)S(1)} %get-tuple-element.109), channel_id=1, source_target_pairs={{0,8},{2,10},{4,12},{6,14},{8,0},{10,2},{12,4},{14,6},{1,9},{3,11}... | collective-permute-start | bytes 417800 | tf_op jit(solution)/shard_map/cond/branch_0_fun/ppermute | solution.py:229
  70.6 3.6 %collective-permute-start.6 = (f16[17,32,128]{2,1,0:T(8,128)(2,1)S(1)}, f16[17,32,128]{2,1,0:T(8,128)(2,1)S(1)}, u32[]{:S(2)}, u32[]{:S(2)}) collective-permute-start(f16[17,32,128]{2,1,0:T(8,128)(2,1)S(1)} %get-tuple-element.108), channel_id=1, source_target_pairs={{0,12},{2,14},{4,0},{6,2},{8,4},{10,6},{12,8},{14,10},{1,13},{3,15... | collective-permute-start | bytes 417800 | tf_op jit(solution)/shard_map/cond/branch_0_fun/ppermute | solution.py:229
  74.2 1.9 %collective-permute-start.7 = (bf16[8,32,512]{2,1,0:T(8,128)(2,1)S(1)}, bf16[8,32,512]{2,1,0:T(8,128)(2,1)}, u32[]{:S(2)}, u32[]{:S(2)}) collective-permute-start(bf16[8,32,512]{2,1,0:T(8,128)(2,1)S(1)} %copy-done.4), channel_id=1, source_target_pairs={{0,16},{16,32},{32,48},{48,64},{64,80},{80,96},{96,112},{112,128},... | collective-permute-start | bytes 786440 | tf_op jit(solution)/shard_map/cond/branch_0_fun/ppermute | solution.py:282
  76.1 6.0 %collective-permute-start.8 = (bf16[8,32,512]{2,1,0:T(8,128)(2,1)S(1)}, bf16[8,32,512]{2,1,0:T(8,128)(2,1)}, u32[]{:S(2)}, u32[]{:S(2)}) collective-permute-start(bf16[8,32,512]{2,1,0:T(8,128)(2,1)S(1)} %copy-done.4), channel_id=1, source_target_pairs={{16,0},{32,16},{48,32},{64,48},{80,64},{96,80},{112,96},{128,112},... | collective-permute-start | bytes 786440 | tf_op jit(solution)/shard_map/cond/branch_0_fun/ppermute | solution.py:283
  82.2 2.7 %collective-permute-done.6 = f16[17,32,128]{2,1,0:T(8,128)(2,1)S(1)} collective-permute-done((f16[17,32,128]{2,1,0:T(8,128)(2,1)S(1)}, f16[17,32,128]{2,1,0:T(8,128)(2,1)S(1)}, u32[]{:S(2)}, u32[]{:S(2)}) %collective-permute-start.6) | collective-permute-done | bytes 139296 | tf_op jit(solution)/shard_map/cond/branch_0_fun/ppermute | solution.py:229
  85.0 1.5 %gather_fusion.1 = f16[64,32,128]{2,1,0:T(8,128)(2,1)} fusion(f16[17,32,128]{2,1,0:T(8,128)(2,1)S(1)} %fusion.2, s32[1024]{0:T(1024)S(1)} %pad_clamp_fusion), kind=kCustom, calls=%fused_computation.1 | custom fusion | bytes 1048832 | tf_op jit(solution)/shard_map/cond/branch_0_fun/jit(_take)/gather | solution.py:290
  86.5 7.4 %all-to-all-start.1 = ((f16[16,4,32,128]{3,2,1,0:T(8,128)(2,1)}), f16[16,4,32,128]{3,2,1,0:T(8,128)(2,1)S(1)}, u32[]{:S(2)}, u32[]{:S(2)}) async-start(f16[16,4,32,128]{3,2,1,0:T(8,128)(2,1)} %bitcast.23), calls=%async_computation.1 | async-start | bytes 1048576 | tf_op jit(solution)/shard_map/all_to_all | solution.py:295
  94.0 0.7 dynamic_slice.3
  94.8 2.3 %base.1 = f32[8,32,512]{2,1,0:T(8,128)S(1)} custom-call(s32[4]{0:T(128)S(1)} %pad_add_fusion.where, s32[128]{0:T(128)S(1)} %copy-done.7, s32[8,4]{1,0:T(8,128)S(1)} %copy.11.neighbors, bf16[8,32,512]{2,1,0:T(8,128)(2,1)} %get-tuple-element.95.low, bf16[8,32,512]{2,1,0:T(8,128)(2,1)} %own.1, bf16[8,32,512]{2,1,0:T(8,128)(2,1)} %get-tuple-element.96.high, ...), custom_call_target="tpu_custom_call" | custom-call | tf_op jit(solution)/shard_map/base/pallas_call | solution.py:296
  97.1 4.8 %all-to-all-done.1 = f16[16,4,32,128]{3,2,1,0:T(8,128)(2,1)S(1)} async-done(((f16[16,4,32,128]{3,2,1,0:T(8,128)(2,1)}), f16[16,4,32,128]{3,2,1,0:T(8,128)(2,1)S(1)}, u32[]{:S(2)}, u32[]{:S(2)}) %all-to-all-start.1) | async-done | bytes 524320 | tf_op jit(solution)/shard_map/all_to_all | solution.py:295
  101.8 0.7 gather_fusion.6
  102.5 1.0 fusion.9
  (38 shorter events, 3.3 us)
Async XLA Ops:
  2.2 16.8 %all-to-all-start = ((bf16[16,4,32,128]{3,2,1,0:T(8,128)(2,1)}), bf16[16,4,32,128]{3,2,1,0:T(8,128)(2,1)S(1)}, u32[]{:S(2)}, u32[]{:S(2)}) async-start(bf16[16,4,32,128]{3,2,1,0:T(8,128)(2,1)} %get-tuple-element.92), calls=%async_computation | async-start | bytes 1048576 | tf_op jit(solution)/shard_map/all_to_all | solution.py:243
  19.0 74.9 %copy-start.14 = (s32[8,4]{0,1:T(4,128)S(1)}, s32[8,4]{0,1:T(4,128)}, u32[]{:S(2)}) copy-start(s32[8,4]{0,1:T(4,128)} %param.11) | copy-start | bytes 388
  19.0 75.7 %copy-start = (bf16[8,4,32,512]{3,2,1,0:T(8,128)(2,1)S(1)}, bf16[8,4,32,512]{3,2,1,0:T(8,128)(2,1)}, u32[]{:S(2)}) copy-start(bf16[8,4,32,512]{3,2,1,0:T(8,128)(2,1)} %couple.1) | copy-start | bytes 3145732
  19.0 75.8 %copy-start.1 = (bf16[8,32,512]{2,1,0:T(8,128)(2,1)S(1)}, bf16[8,32,512]{2,1,0:T(8,128)(2,1)}, u32[]{:S(2)}) copy-start(bf16[8,32,512]{2,1,0:T(8,128)(2,1)} %hcore.1) | copy-start | bytes 786436
  19.0 75.8 %copy-start.7 = (s32[128]{0:T(128)S(1)}, s32[128]{0:T(128)}, u32[]{:S(2)}) copy-start(s32[128]{0:T(128)} %sizes.5) | copy-start | bytes 1540
  45.8 0.7 copy-start.8
  45.8 0.7 copy-start.11
  53.9 2.0 %collective-permute-start.1 = (f16[4,17,32,128]{3,2,1,0:T(8,128)(2,1)S(1)}, f16[4,17,32,128]{3,2,1,0:T(8,128)(2,1)S(1)}, u32[]{:S(2)}, u32[]{:S(2)}) collective-permute-start(f16[4,17,32,128]{3,2,1,0:T(8,128)(2,1)S(1)} %get-tuple-element.106), channel_id=1, source_target_pairs={{0,1},{1,0},{2,3},{3,2},{4,5},{5,4},{6,7},{7,6},{8,9},{9,8},{10,11... | collective-permute-start | bytes 1671176 | tf_op jit(solution)/shard_map/cond/branch_0_fun/ppermute | solution.py:277
  54.4 5.3 %collective-permute-start = (f16[4,17,32,128]{3,2,1,0:T(8,128)(2,1)S(1)}, f16[4,17,32,128]{3,2,1,0:T(8,128)(2,1)S(1)}, u32[]{:S(2)}, u32[]{:S(2)}) collective-permute-start(f16[4,17,32,128]{3,2,1,0:T(8,128)(2,1)S(1)} %get-tuple-element.105), channel_id=1, source_target_pairs={{0,1},{1,0},{2,3},{3,2},{4,5},{5,4},{6,7},{7,6},{8,9},{9,8},{10,11... | collective-permute-start | bytes 1671176 | tf_op jit(solution)/shard_map/cond/branch_0_fun/ppermute | solution.py:277
  56.3 10.6 %collective-permute-start.2 = (f16[4,9,32,128]{3,2,1,0:T(8,128)(2,1)S(1)}, f16[4,9,32,128]{3,2,1,0:T(8,128)(2,1)S(1)}, u32[]{:S(2)}, u32[]{:S(2)}) collective-permute-start(f16[4,9,32,128]{3,2,1,0:T(8,128)(2,1)S(1)} %slice.126), channel_id=1, source_target_pairs={{0,2},{2,4},{4,6},{6,8},{8,10},{10,12},{12,14},{14,0},{1,3},{3,5},... | collective-permute-start | bytes 884744 | tf_op jit(solution)/shard_map/cond/branch_0_fun/ppermute | solution.py:229
  57.2 17.0 %copy-start.4 = (bf16[8,32,512]{2,1,0:T(8,128)(2,1)S(1)}, bf16[8,32,512]{2,1,0:T(8,128)(2,1)}, u32[]{:S(2)}) copy-start(bf16[8,32,512]{2,1,0:T(8,128)(2,1)} %get-tuple-element.62) | copy-start | bytes 786436 | tf_op jit(solution)/shard_map/cond
  57.2 8.4 %collective-permute-start.3 = (f16[4,8,32,128]{3,2,1,0:T(8,128)(2,1)S(1)}, f16[4,8,32,128]{3,2,1,0:T(8,128)(2,1)S(1)}, u32[]{:S(2)}, u32[]{:S(2)}) collective-permute-start(f16[4,8,32,128]{3,2,1,0:T(8,128)(2,1)S(1)} %slice.127), channel_id=1, source_target_pairs={{0,14},{2,0},{4,2},{6,4},{8,6},{10,8},{12,10},{14,12},{1,15},{3,1}... | collective-permute-start | bytes 786440 | tf_op jit(solution)/shard_map/cond/branch_0_fun/ppermute | solution.py:229
  67.3 14.9 %collective-permute-start.4 = (f16[17,32,128]{2,1,0:T(8,128)(2,1)S(1)}, f16[17,32,128]{2,1,0:T(8,128)(2,1)S(1)}, u32[]{:S(2)}, u32[]{:S(2)}) collective-permute-start(f16[17,32,128]{2,1,0:T(8,128)(2,1)S(1)} %get-tuple-element.107), channel_id=1, source_target_pairs={{0,4},{2,6},{4,8},{6,10},{8,12},{10,14},{12,0},{14,2},{1,5},{3,7},... | collective-permute-start | bytes 417800 | tf_op jit(solution)/shard_map/cond/branch_0_fun/ppermute | solution.py:229
  67.4 14.8 %collective-permute-start.5 = (f16[17,32,128]{2,1,0:T(8,128)(2,1)S(1)}, f16[17,32,128]{2,1,0:T(8,128)(2,1)S(1)}, u32[]{:S(2)}, u32[]{:S(2)}) collective-permute-start(f16[17,32,128]{2,1,0:T(8,128)(2,1)S(1)} %get-tuple-element.109), channel_id=1, source_target_pairs={{0,8},{2,10},{4,12},{6,14},{8,0},{10,2},{12,4},{14,6},{1,9},{3,11}... | collective-permute-start | bytes 417800 | tf_op jit(solution)/shard_map/cond/branch_0_fun/ppermute | solution.py:229
  70.6 14.3 %collective-permute-start.6 = (f16[17,32,128]{2,1,0:T(8,128)(2,1)S(1)}, f16[17,32,128]{2,1,0:T(8,128)(2,1)S(1)}, u32[]{:S(2)}, u32[]{:S(2)}) collective-permute-start(f16[17,32,128]{2,1,0:T(8,128)(2,1)S(1)} %get-tuple-element.108), channel_id=1, source_target_pairs={{0,12},{2,14},{4,0},{6,2},{8,4},{10,6},{12,8},{14,10},{1,13},{3,15... | collective-permute-start | bytes 417800 | tf_op jit(solution)/shard_map/cond/branch_0_fun/ppermute | solution.py:229
  74.2 12.3 %collective-permute-start.7 = (bf16[8,32,512]{2,1,0:T(8,128)(2,1)S(1)}, bf16[8,32,512]{2,1,0:T(8,128)(2,1)}, u32[]{:S(2)}, u32[]{:S(2)}) collective-permute-start(bf16[8,32,512]{2,1,0:T(8,128)(2,1)S(1)} %copy-done.4), channel_id=1, source_target_pairs={{0,16},{16,32},{32,48},{48,64},{64,80},{80,96},{96,112},{112,128},... | collective-permute-start | bytes 786440 | tf_op jit(solution)/shard_map/cond/branch_0_fun/ppermute | solution.py:282
  76.1 10.4 %collective-permute-start.8 = (bf16[8,32,512]{2,1,0:T(8,128)(2,1)S(1)}, bf16[8,32,512]{2,1,0:T(8,128)(2,1)}, u32[]{:S(2)}, u32[]{:S(2)}) collective-permute-start(bf16[8,32,512]{2,1,0:T(8,128)(2,1)S(1)} %copy-done.4), channel_id=1, source_target_pairs={{16,0},{32,16},{48,32},{64,48},{80,64},{96,80},{112,96},{128,112},... | collective-permute-start | bytes 786440 | tf_op jit(solution)/shard_map/cond/branch_0_fun/ppermute | solution.py:283
  86.5 15.3 %all-to-all-start.1 = ((f16[16,4,32,128]{3,2,1,0:T(8,128)(2,1)}), f16[16,4,32,128]{3,2,1,0:T(8,128)(2,1)S(1)}, u32[]{:S(2)}, u32[]{:S(2)}) async-start(f16[16,4,32,128]{3,2,1,0:T(8,128)(2,1)} %bitcast.23), calls=%async_computation.1 | async-start | bytes 1048576 | tf_op jit(solution)/shard_map/all_to_all | solution.py:295
